TPU v7x, 32 devices: a whole 2x2x4 slice. The times are simulated.
32 devices in a mesh: rep: 8 (over z, core), exp: 4 (over y, x).
Axes of the slice: x: 2, y: 2, z: 4, core: 2. Of those that a mesh axis runs over, the one named last changes fastest.
Arguments:
- latents: float32 [16, 32, 2048], P('rep', None, 'exp'), may hold values from -6 to 6
- latent_mean: float32 [16, 32, 2048], P('rep', None, 'exp'), may hold values from -0.12 to 0.12
- latent_square: float32 [16, 32, 2048], P('rep', None, 'exp'), may hold values from 0.0001 to 0.01
- weight_one: bfloat16 [16, 64, 256], P('exp'), may hold values from -0.75 to 0.75
- weight_two: bfloat16 [16, 256, 256], P('exp'), may hold values from -0.375 to 0.375
- weight_three: bfloat16 [16, 3, 256], P('exp'), may hold values from -0.375 to 0.375
- dir_table: bfloat16 [256, 32], replicated, may hold values from -6 to 6
- materials: int32 [65536, 1], P(('rep', 'exp')), may hold values from 0 to 15; in each aligned block of 2048 rows (0 to 2047, 2048 to 4095, ...) at most 256 rows name the same one
- tile_ids: int32 [65536], P(('rep', 'exp')), may hold values from 0 to 1
- texel_ids: int32 [65536], P(('rep', 'exp')), may hold values from 0 to 2047
- dir_ids: int32 [65536], P(('rep', 'exp')), may hold values from 0 to 255
- targets: float32 [3, 65536], P(None, ('rep', 'exp')), may hold values from -12 to 12
Outputs:
- new_latents: float32 [16, 32, 2048], P('rep', None, 'exp')
- new_mean: float32 [16, 32, 2048], P('rep', None, 'exp')
- new_square: float32 [16, 32, 2048], P('rep', None, 'exp')
- predictions: float32 [3, 65536], P(None, ('rep', 'exp'))
- grad_one: float32 [16, 64, 256], P('exp')
- grad_two: float32 [16, 256, 256], P('exp')
- grad_three: float32 [16, 3, 256], P('exp')
Inputs may be any that keep to these rules, and one draw needn't show every extreme that they name: `materials`: within the rows of one device no material is named by more than 256 rows, a bound that some block reaches.
All inputs are finite; a program needn't handle non-finite values.
Results may differ from a plain program's by a relative error of at most 0.02.
Values may be sent and summed in bfloat16 or wider, within the bound.
A program may use at most 64 MiB of HBM per device.

v0:
```python
import jax
import jax.numpy as jnp
from jax import lax
from jax.sharding import PartitionSpec as P

LAT = 32
OUTC = 3


decay_one = 0.9
decay_two = 0.99
step_rate = 0.05
epsilon = 1e-08


def silu_slope(preact):
    sigmoid_v = jax.nn.sigmoid(preact)
    return sigmoid_v * (1.0 + preact * (1.0 - sigmoid_v))


def expert_step(inputs, target_rows, layer_one, layer_two, layer_three):
    pre_one = jnp.dot(inputs, layer_one, preferred_element_type=jnp.float32)
    act_one = jax.nn.silu(pre_one).astype(jnp.bfloat16)
    pre_two = jnp.dot(act_one, layer_two, preferred_element_type=jnp.float32)
    act_two = jax.nn.silu(pre_two).astype(jnp.bfloat16)
    predicted = lax.dot_general(
        act_two, layer_three, (((1,), (1,)), ((), ())), preferred_element_type=jnp.float32
    )
    misfit = (predicted - target_rows).astype(jnp.bfloat16)
    grad_three = lax.dot_general(
        misfit, act_two, (((0,), (0,)), ((), ())), preferred_element_type=jnp.float32
    )
    back_two = jnp.dot(misfit, layer_three, preferred_element_type=jnp.float32)
    delta_two = (back_two * silu_slope(pre_two)).astype(jnp.bfloat16)
    grad_two = lax.dot_general(
        act_one, delta_two, (((0,), (0,)), ((), ())), preferred_element_type=jnp.float32
    )
    back_one = lax.dot_general(
        delta_two, layer_two, (((1,), (1,)), ((), ())), preferred_element_type=jnp.float32
    )
    delta_one = (back_one * silu_slope(pre_one)).astype(jnp.bfloat16)
    grad_one = lax.dot_general(
        inputs, delta_one, (((0,), (0,)), ((), ())), preferred_element_type=jnp.float32
    )
    latent_part = layer_one[:LAT]
    latent_rows = lax.dot_general(
        delta_one, latent_part, (((1,), (1,)), ((), ())), preferred_element_type=jnp.float32
    )
    return (latent_rows.astype(jnp.bfloat16), predicted, grad_one, grad_two, grad_three)


def direction_rows(entries, dir_table):
    table_hot = (
        entries[:, None] == jnp.arange(dir_table.shape[0], dtype=jnp.int32)[None, :]
    ).astype(jnp.bfloat16)
    return jnp.dot(table_hot, dir_table, preferred_element_type=jnp.float32).astype(jnp.bfloat16)


def on_device(
    latents,
    latent_mean,
    latent_square,
    weight_one,
    weight_two,
    weight_three,
    dir_table,
    materials,
    tile_ids,
    texel_ids,
    dir_ids,
    targets,
):
    exp_count = lax.axis_size("exp")
    local_experts = weight_one.shape[0]
    total_experts = local_experts * exp_count
    samples = materials.shape[0]
    capacity = 2 * samples // total_experts
    total_slots = total_experts * capacity
    latent_bf = latents.astype(jnp.bfloat16)
    texture = lax.all_gather(latent_bf, "exp", axis=2, tiled=True)
    sample_latent = texture[tile_ids, :, texel_ids]
    material = materials[:, 0]
    one_hot = (material[:, None] == jnp.arange(total_experts, dtype=jnp.int32)[None, :]).astype(
        jnp.int32
    )
    position = jnp.sum((jnp.cumsum(one_hot, axis=0) - 1) * one_hot, axis=1)
    owner_dev = material // local_experts
    within = material % local_experts
    slot_index = (within * exp_count + owner_dev) * capacity + position
    send_targets = jnp.zeros((total_slots, OUTC), jnp.float32).at[slot_index].set(targets.T)
    send_targets = send_targets.reshape(local_experts, exp_count, capacity * OUTC)
    feature_rows = jnp.concatenate([sample_latent, direction_rows(dir_ids, dir_table)], axis=1)
    width = feature_rows.shape[1]
    send_rows = jnp.zeros((total_slots, width), jnp.bfloat16).at[slot_index].set(feature_rows)
    send_rows = send_rows.reshape(local_experts, exp_count, capacity * width)
    got_rows, got_targets = (
        lax.all_to_all(send_rows, "exp", split_axis=1, concat_axis=1, tiled=True),
        lax.all_to_all(
            send_targets.astype(jnp.bfloat16), "exp", split_axis=1, concat_axis=1, tiled=True
        ).astype(send_targets.dtype),
    )
    inputs = got_rows.reshape(local_experts, exp_count * capacity, width)
    wanted = got_targets.reshape(local_experts, exp_count * capacity, OUTC)

    def run_expert(packed):
        return expert_step(packed[0], packed[1], packed[2], packed[3], packed[4])

    latent_rows, predicted, grad_one, grad_two, grad_three = lax.map(
        run_expert, (inputs, wanted, weight_one, weight_two, weight_three)
    )
    back_latent, back_pred = (
        lax.all_to_all(
            latent_rows.reshape(local_experts, exp_count, capacity * LAT),
            "exp",
            split_axis=1,
            concat_axis=1,
            tiled=True,
        ),
        lax.all_to_all(
            predicted.reshape(local_experts, exp_count, capacity * OUTC).astype(jnp.bfloat16),
            "exp",
            split_axis=1,
            concat_axis=1,
            tiled=True,
        ).astype(jnp.float32),
    )
    grad_one, grad_two, grad_three = (
        lax.psum(grad_one.astype(jnp.bfloat16), "rep").astype(jnp.float32),
        lax.psum(grad_two.astype(jnp.bfloat16), "rep").astype(jnp.float32),
        lax.psum(grad_three.astype(jnp.bfloat16), "rep").astype(jnp.float32),
    )
    sample_grad = back_latent.reshape(total_slots, LAT)[slot_index].astype(jnp.float32)
    sample_pred = back_pred.reshape(total_slots, OUTC)[slot_index]
    dense_grad = jnp.zeros(texture.shape, jnp.float32).at[tile_ids, :, texel_ids].add(sample_grad)
    texel_grad = lax.psum_scatter(
        dense_grad.astype(jnp.bfloat16), "exp", scatter_dimension=2, tiled=True
    ).astype(jnp.float32)
    new_mean = decay_one * latent_mean + (1.0 - decay_one) * texel_grad
    new_square = decay_two * latent_square + (1.0 - decay_two) * texel_grad * texel_grad
    new_latents = latents - step_rate * new_mean / (jnp.sqrt(new_square) + epsilon)
    return (new_latents, new_mean, new_square, sample_pred.T, grad_one, grad_two, grad_three)


def solution(mesh):
    in_specs = (
        P("rep", None, "exp"),
        P("rep", None, "exp"),
        P("rep", None, "exp"),
        P("exp", None, None),
        P("exp", None, None),
        P("exp", None, None),
        P(),
        P(("rep", "exp"), None),
        P(("rep", "exp")),
        P(("rep", "exp")),
        P(("rep", "exp")),
        P(None, ("rep", "exp")),
    )
    out_specs = (
        P("rep", None, "exp"),
        P("rep", None, "exp"),
        P("rep", None, "exp"),
        P(None, ("rep", "exp")),
        P("exp", None, None),
        P("exp", None, None),
        P("exp", None, None),
    )
    return jax.shard_map(
        on_device, mesh=mesh, in_specs=in_specs, out_specs=out_specs, check_vma=False
    )
```

profile of v0, /device:TPU:0, one launch (start us, length us, event | category | flops | bytes accessed | tf_op | source)
XLA Modules:
  0.0 250.0 jit_solution(13107071563818476497)
XLA Ops:
  8.7 4.5 %reduce-window.6 = s32[16,16,128]{2,1,0:T(8,128)S(1)} reduce-window(s32[16,16,128]{2,1,0:T(8,128)S(1)} %fusion.40, s32[]{:T(128)} %constant.51.clone.1), window={size=1x1x128 pad=0_0x0_0x127_0}, to_apply=%region_0.0 | reduce-window | flops 4161536 | bytes 262148 | tf_op jit(solution)/shard_map/reduce-window
  16.7 6.1 %scatter_custom_fusion.1 = f32[4096,3]{1,0:T(8,128)S(1)} fusion(s32[2048]{0:T(1024)S(1)} %bitcast.142, f32[2048,3]{1,0:T(8,128)S(1)} %copy.87, f32[]{:T(128)} %constant.49.clone.1), kind=kCustom, calls=%fused_computation.51 | custom fusion | bytes 49156 | tf_op jit(solution)/shard_map/scatter | solution.py:90
  24.9 5.2 %all-to-all-start.1 = ((bf16[4,4,768]{2,0,1:T(4,128)(2,1)}), bf16[4,4,768]{2,0,1:T(4,128)(2,1)S(1)}, u32[]{:S(2)}, u32[]{:S(2)}) async-start(bf16[4,4,768]{2,0,1:T(4,128)(2,1)} %copy.88), calls=%async_computation.1 | async-start | bytes 49152 | tf_op jit(solution)/shard_map/all_to_all | solution.py:98
  30.1 9.5 %all_gather.3 = bf16[2,32,2048]{2,1,0:T(8,128)(2,1)S(1)} all-gather(bf16[2,32,512]{2,1,0:T(8,128)(2,1)S(1)} %convert_element_type.72), channel_id=1, replica_groups=mesh['rep'=8,'exp'=4] {'exp'}, dimensions={2}, use_global_device_ids=true | all-gather | bytes 327680 | tf_op jit(solution)/shard_map/all_gather | solution.py:80
  40.2 11.1 %gather_fusion = bf16[2048,32]{1,0:T(8,128)(2,1)S(1)} fusion(bf16[2,32,2048]{1,2,0:T(8,128)(2,1)S(1)} %copy.82, s32[2048]{0:T(1024)S(1)} %bitcast.126), kind=kCustom, calls=%fused_computation | custom fusion | bytes 278528 | tf_op jit(solution)/shard_map/gather | solution.py:81
  52.3 6.1 %scatter_custom_fusion = bf16[4096,64]{1,0:T(8,128)(2,1)S(1)} fusion(s32[2048]{0:T(1024)S(1)} %bitcast.143, bf16[2048,64]{1,0:T(8,128)(2,1)S(1)} %copy.84, bf16[]{:T(256)} %constant.57.clone.1), kind=kCustom, calls=%fused_computation.54 | custom fusion | bytes 524290 | tf_op jit(solution)/shard_map/scatter | solution.py:94
  60.4 3.5 %all-to-all-start = ((bf16[4,4,16384]{2,0,1:T(4,128)(2,1)}), bf16[4,4,16384]{2,0,1:T(4,128)(2,1)S(1)}, u32[]{:S(2)}, u32[]{:S(2)}) async-start(bf16[4,4,16384]{2,0,1:T(4,128)(2,1)} %copy.85), calls=%async_computation | async-start | bytes 1048576 | tf_op jit(solution)/shard_map/all_to_all | solution.py:97
  64.4 2.0 reshape.77
  67.0 3.4 %all-to-all-done = bf16[4,4,16384]{2,0,1:T(4,128)(2,1)S(1)} async-done(((bf16[4,4,16384]{2,0,1:T(4,128)(2,1)}), bf16[4,4,16384]{2,0,1:T(4,128)(2,1)S(1)}, u32[]{:S(2)}, u32[]{:S(2)}) %all-to-all-start) | async-done | bytes 524320 | tf_op jit(solution)/shard_map/all_to_all | solution.py:97
  71.6 32.2 %while.18 = (s32[]{:T(128)}, bf16[4,1024,32]{1,2,0:T(8,128)(2,1)S(1)}, bf16[4,1024,3]{1,2,0:T(4,128)(2,1)S(1)}, bf16[4,64,256]{2,1,0:T(8,128)(2,1)S(1)}, bf16[4,...) while((s32[]{:T(128)}, ...), condition=%wide.region_6.7_spmd, body=%wide.region_5.6_spmd.sunk | while | flops 499950592 | bytes 12314269 | solution.py:108
  72.7 1.5 multiply_convert_fusion.7
  75.0 1.4 fusion.91
  80.7 1.5 multiply_convert_fusion.7
  83.0 1.4 fusion.91
  88.8 1.5 multiply_convert_fusion.7
  91.1 1.4 fusion.91
  96.8 1.5 multiply_convert_fusion.7
  99.1 1.4 fusion.91
  107.1 3.4 %all-to-all-start.2 = ((bf16[4,4,8192]{2,0,1:T(4,128)(2,1)}), bf16[4,4,8192]{2,0,1:T(4,128)(2,1)S(1)}, u32[]{:S(2)}, u32[]{:S(2)}) async-start(bf16[4,4,8192]{2,0,1:T(4,128)(2,1)} %copy.93), calls=%async_computation.2 | async-start | bytes 524288 | tf_op jit(solution)/shard_map/all_to_all | solution.py:112
  110.6 5.3 %all-to-all-done.2 = bf16[4,4,8192]{2,0,1:T(4,128)(2,1)S(1)} async-done(((bf16[4,4,8192]{2,0,1:T(4,128)(2,1)}), bf16[4,4,8192]{2,0,1:T(4,128)(2,1)S(1)}, u32[]{:S(2)}, u32[]{:S(2)}) %all-to-all-start.2) | async-done | bytes 262176 | tf_op jit(solution)/shard_map/all_to_all | solution.py:112
  116.7 18.4 %scatter_custom_fusion.2 = f32[4096,32]{1,0:T(8,128)S(1)} fusion(s32[2048]{0:T(1024)S(1)} %broadcast_select_fusion, f32[]{:T(128)} %constant.49.clone.1, bf16[4096,32]{1,0:T(8,128)(2,1)S(1)} %reshape.69, s32[2048]{0:T(1024)S(1)} %broadcast_clamp_fusion), kind=kCustom, calls=%fused_computation.48 | custom fusion | flops 131072 | bytes 1581060
  135.5 26.5 %copy.102 = bf16[2,32,2048]{0,1,2:T(8,128)(2,1)} copy(bf16[2,32,2048]{2,0,1:T(2,128)(2,1)S(1)} %bitcast.130) | data formatting | bytes 524288
  162.0 31.8 %reshape.125 = bf16[2048,64]{1,0:T(8,128)(2,1)} reshape(bf16[2048,32,2]{2,1,0:T(8,128)(2,1)} %bitcast.127) | data formatting | bytes 524288
  194.3 1.4 convert_element_type.80
  196.3 3.3 %all-to-all-start.3 = ((bf16[4,4,768]{2,0,1:T(4,128)(2,1)}), bf16[4,4,768]{2,0,1:T(4,128)(2,1)S(1)}, u32[]{:S(2)}, u32[]{:S(2)}) async-start(bf16[4,4,768]{2,0,1:T(4,128)(2,1)} %copy.98), calls=%async_computation.3 | async-start | bytes 49152 | tf_op jit(solution)/shard_map/all_to_all | solution.py:119
  199.6 13.8 %psum.23 = bf16[4,3,256]{2,0,1:T(4,128)(2,1)S(1)} all-reduce(bf16[4,3,256]{2,0,1:T(4,128)(2,1)S(1)} %copy-done.10), channel_id=1, replica_groups=mesh['rep'=8,'exp'=4] {'rep'}, use_global_device_ids=true, to_apply=%region_11.12 | all-reduce | flops 3072 | bytes 12288 | tf_op jit(solution)/shard_map/psum | solution.py:130
  214.1 2.0 reshape.79
  216.1 5.5 %gather_fusion.1 = f32[2048,3]{1,0:T(8,128)S(1)} fusion(f32[4096,3]{1,0:T(8,128)S(1)} %reshape.79, s32[2048]{0:T(1024)S(1)} %broadcast_clamp_fusion), kind=kCustom, calls=%fused_computation.2 | custom fusion | bytes 57344 | tf_op jit(solution)/shard_map/gather | solution.py:133
  222.5 1.6 convert_element_type.82
  224.1 2.1 convert_element_type.84
  226.2 10.7 %reshape.126 = bf16[512,32,2]{2,1,0:T(8,128)(2,1)} reshape(bf16[512,64]{1,0:T(8,128)(2,1)} %reduce-scatter.4.cloned.1.call-done) | data formatting | bytes 131072
  236.9 4.8 %copy.96 = bf16[2,32,512]{2,1,0:T(8,128)(2,1)S(1)} copy(bf16[2,32,512]{0,1,2:T(8,128)(2,1)} %bitcast.128) | data formatting | bytes 131072 | tf_op jit(solution)/shard_map/reduce_scatter | solution.py:135
  (124 shorter events, 40.4 us)
Async XLA Ops:
  8.0 43.5 %copy-start = (bf16[256,32]{0,1:T(8,128)(2,1)S(1)}, bf16[256,32]{0,1:T(8,128)(2,1)}, u32[]{:S(2)}) copy-start(bf16[256,32]{0,1:T(8,128)(2,1)} %param.20) | copy-start | bytes 49156
  22.8 7.3 %copy-start.7 = (s32[2048]{0:T(1024)S(1)}, s32[2048]{0:T(1024)}, u32[]{:S(2)}) copy-start(s32[2048]{0:T(1024)} %param.23) | copy-start | bytes 24580
  22.8 7.3 %copy-start.8 = (s32[2048]{0:T(1024)S(1)}, s32[2048]{0:T(1024)}, u32[]{:S(2)}) copy-start(s32[2048]{0:T(1024)} %param.22) | copy-start | bytes 24580
  22.8 7.3 %copy-start.2 = (f32[2,32,512]{2,1,0:T(8,128)S(1)}, f32[2,32,512]{2,1,0:T(8,128)}, u32[]{:S(2)}) copy-start(f32[2,32,512]{2,1,0:T(8,128)} %param.14) | copy-start | bytes 393220
  24.9 35.5 %all-to-all-start.1 = ((bf16[4,4,768]{2,0,1:T(4,128)(2,1)}), bf16[4,4,768]{2,0,1:T(4,128)(2,1)S(1)}, u32[]{:S(2)}, u32[]{:S(2)}) async-start(bf16[4,4,768]{2,0,1:T(4,128)(2,1)} %copy.88), calls=%async_computation.1 | async-start | bytes 49152 | tf_op jit(solution)/shard_map/all_to_all | solution.py:98
  40.2 11.3 %copy-start.13 = (s32[2048]{0:T(1024)S(1)}, s32[2048]{0:T(1024)}, u32[]{:S(2)}) copy-start(s32[2048]{0:T(1024)} %param.24) | copy-start | bytes 24580
  58.4 5.7 %copy-start.9 = (bf16[4,3,256]{2,0,1:T(4,128)(2,1)S(1)}, bf16[4,3,256]{2,0,1:T(4,128)(2,1)}, u32[]{:S(2)}) copy-start(bf16[4,3,256]{2,0,1:T(4,128)(2,1)} %param.19) | copy-start | bytes 18436
  58.4 5.7 %copy-start.12 = (s32[2]{0:T(128)S(1)}, s32[2]{0:T(128)}, u32[]{:S(2)}) copy-start(s32[2]{0:T(128)} %constant.99) | copy-start | bytes 28
  58.4 5.8 %copy-start.11 = (s32[2]{0:T(128)S(1)}, s32[2]{0:T(128)}, u32[]{:S(2)}) copy-start(s32[2]{0:T(128)} %constant.102) | copy-start | bytes 28
  60.4 10.0 %all-to-all-start = ((bf16[4,4,16384]{2,0,1:T(4,128)(2,1)}), bf16[4,4,16384]{2,0,1:T(4,128)(2,1)S(1)}, u32[]{:S(2)}, u32[]{:S(2)}) async-start(bf16[4,4,16384]{2,0,1:T(4,128)(2,1)} %copy.85), calls=%async_computation | async-start | bytes 1048576 | tf_op jit(solution)/shard_map/all_to_all | solution.py:97
  63.9 158.6 %all-reduce.3.cloned.1.call-start = ((), (), s32[]{:S(2)}) async-start(), calls=%async_computation.6 | async-start | bytes 1310720 | tf_op jit(solution)/shard_map/psum | solution.py:128
  67.0 4.6 %copy-start.3 = (bf16[4,1024,32]{1,2,0:T(8,128)(2,1)S(1)}, bf16[4,1024,32]{1,2,0:T(8,128)(2,1)}, u32[]{:S(2)}) copy-start(bf16[4,1024,32]{1,2,0:T(8,128)(2,1)} %custom-call.6) | copy-start | bytes 786436
  103.8 0.8 copy-start.1
  103.8 0.8 copy-start.4
  107.1 8.8 %all-to-all-start.2 = ((bf16[4,4,8192]{2,0,1:T(4,128)(2,1)}), bf16[4,4,8192]{2,0,1:T(4,128)(2,1)S(1)}, u32[]{:S(2)}, u32[]{:S(2)}) async-start(bf16[4,4,8192]{2,0,1:T(4,128)(2,1)} %copy.93), calls=%async_computation.2 | async-start | bytes 524288 | tf_op jit(solution)/shard_map/all_to_all | solution.py:112
  110.5 115.7 %reduce-scatter.4.cloned.1.call-start = ((), (), s32[]{:S(2)}) async-start(), calls=%async_computation.5 | async-start | bytes 655360
  193.8 5.8 %copy-start.10 = (bf16[4,3,256]{2,0,1:T(4,128)(2,1)S(1)}, bf16[4,3,256]{2,0,1:T(4,128)(2,1)}, u32[]{:S(2)}) copy-start(bf16[4,3,256]{2,0,1:T(4,128)(2,1)} %get-tuple-element.72) | copy-start | bytes 18436
  196.3 17.7 %all-to-all-start.3 = ((bf16[4,4,768]{2,0,1:T(4,128)(2,1)}), bf16[4,4,768]{2,0,1:T(4,128)(2,1)S(1)}, u32[]{:S(2)}, u32[]{:S(2)}) async-start(bf16[4,4,768]{2,0,1:T(4,128)(2,1)} %copy.98), calls=%async_computation.3 | async-start | bytes 49152 | tf_op jit(solution)/shard_map/all_to_all | solution.py:119
  236.9 4.9 %copy-start.5 = (f32[2,32,512]{2,1,0:T(8,128)S(1)}, f32[2,32,512]{2,1,0:T(8,128)}, u32[]{:S(2)}) copy-start(f32[2,32,512]{2,1,0:T(8,128)} %param.15) | copy-start | bytes 393220
  236.9 4.9 %copy-start.6 = (f32[2,32,512]{2,1,0:T(8,128)S(1)}, f32[2,32,512]{2,1,0:T(8,128)}, u32[]{:S(2)}) copy-start(f32[2,32,512]{2,1,0:T(8,128)} %param.16) | copy-start | bytes 393220
Sparse Core Ops, SparseCore 0:
  104.8 57.4 all-reduce.2
Sparse Core Ops, SparseCore 1:
  193.9 25.1 reduce-scatter.3
where the time goes:
time: 252 us; the launch traced here: 250 us
  local copies, waits for them, and re-layouts  128 us (51%)
  other arithmetic  30.9 us (12%)
  matrix products  27.1 us (11%)
  blocking collectives  23.3 us (9%)
  between operations  15.9 us (6%)
  starting transfers between devices  15.6 us (6%)
  waiting for transfers between devices  8.7 us (3%)
    unnamed x33, local copies, waits for them, and re-layouts  71.1 us
    unnamed x4, other arithmetic  18.6 us
    psum x1, blocking collectives, on_device(): lax.psum(grad_three.astype(jnp.bfloat16), 'rep').astype(jnp.float32)  13.8 us
    gather x2, local copies, waits for them, and re-layouts, on_device(): sample_latent = texture[tile_ids, :, texel_ids]  11.3 us
    all_gather x1, blocking collectives, on_device(): texture = lax.all_gather(latent_bf, 'exp', axis=2, tiled=True)  9.49 us
    scatter x1, local copies, waits for them, and re-layouts, on_device(): jnp.zeros((total_slots, OUTC), jnp.float32).at[slot_index].set(targets.T)  6.1 us
    scatter x1, local copies, waits for them, and re-layouts, on_device(): jnp.zeros((total_slots, width), jnp.bfloat16).at[slot_index]  6.07 us
    dot_general x4, matrix products, expert_step(): pre_two = jnp.dot(act_one, layer_two, preferred_element_type=jnp.float32)  5.92 us
  transfers between devices with their start and end apart: 6, of which 2 were waited for; matrix products, arithmetic and copies ran while one was open for 48% of the time, Pallas kernels for 0%

commit v1 on v0

v1 whole, which is shorter than its diff:
```python
import functools

import jax
import jax.numpy as jnp
from jax import lax
from jax.experimental import pallas as pl
from jax.experimental.pallas import tpu as pltpu
from jax.sharding import PartitionSpec as P

BF = jnp.bfloat16
F32 = jnp.float32
MESH = pl.DeviceIdType.MESH
decay_one = 0.9
decay_two = 0.99
step_rate = 0.05
epsilon = 1e-08
VROWS = 16


def nn(a, b):
    return lax.dot_general(a, b, (((1,), (0,)), ((), ())), preferred_element_type=F32)


def nt(a, b):
    return lax.dot_general(a, b, (((1,), (1,)), ((), ())), preferred_element_type=F32)


def tn(a, b):
    return lax.dot_general(a, b, (((0,), (0,)), ((), ())), preferred_element_type=F32)


def hot(cond):
    return jnp.where(cond, 1.0, 0.0).astype(BF)


def step_kernel(
    cfg,
    lat_ref,
    mean_ref,
    sq_ref,
    w1_ref,
    w2_ref,
    w3_ref,
    dirt_ref,
    mat_ref,
    tile_ref,
    texel_ref,
    dir_ref,
    tgt_ref,
    nlat_ref,
    nmean_ref,
    nsq_ref,
    pred_ref,
    g1_ref,
    g2_ref,
    g3_ref,
    tex,
    slot_send,
    slot_recv,
    q_ref,
    ps_send,
    ps_recv,
    dg_acc,
    dg_send,
    dg_recv,
    g1_acc,
    gfull,
    hs_send,
    hs_recv,
    zs_send,
    zr_recv,
    fin,
    tex_sems,
    slot_sems,
    ps_sems,
    dg_sems,
    hs_sems,
    zr_sems,
    ag_sems,
    fw_sems,
):
    N, R, E, L = cfg["N"], cfg["R"], cfg["E"], cfg["L"]
    S, CAP, HI, LOL, LO = cfg["S"], cfg["CAP"], cfg["HI"], cfg["LOL"], cfg["LO"]
    LAT, DIRF, HID, T, Z = cfg["LAT"], cfg["DIRF"], cfg["HID"], cfg["T"], cfg["Z"]
    OUTC, CH, RC, SB = cfg["OUTC"], cfg["CH"], cfg["RC"], cfg["SB"]
    NDIR = dirt_ref.shape[0]
    PL = LOL * LAT
    K = LO * LAT
    me = lax.axis_index("exp")
    rep = lax.axis_index("rep")
    core = rep % 2
    zi = rep // 2
    mate = zi * 2 + (1 - core)

    def remote(src, dst, sems, index, peer):
        return pltpu.make_async_remote_copy(
            src_ref=src,
            dst_ref=dst,
            send_sem=sems.at[(0,) + index],
            recv_sem=sems.at[(1,) + index],
            device_id=peer,
            device_id_type=MESH,
        )

    barrier = pltpu.get_barrier_semaphore()
    for k in range(1, N):
        pl.semaphore_signal(
            barrier, inc=1, device_id={"exp": (me + k) % N}, device_id_type=MESH
        )
    pl.semaphore_signal(barrier, inc=1, device_id={"rep": mate}, device_id_type=MESH)
    for k in range(1, Z):
        pl.semaphore_signal(
            barrier,
            inc=1,
            device_id={"rep": ((zi + k) % Z) * 2 + core},
            device_id_type=MESH,
        )
    for t in range(T):
        for l in range(LOL):
            tex[me, t, l * LAT : (l + 1) * LAT, :] = lat_ref[
                t, :, l * HI : (l + 1) * HI
            ].astype(BF)
    pl.semaphore_wait(barrier, (N - 1) + 1 + (Z - 1))

    def tex_copy(k):
        return remote(tex.at[me], tex.at[me], tex_sems, (k - 1,), {"exp": (me + k) % N})

    for k in range(1, N):
        tex_copy(k).start()

    mat = mat_ref[...]
    one_hot = jnp.where(
        lax.broadcasted_iota(jnp.int32, (E, S), 0) == mat, 1.0, 0.0
    )
    W = min(256, S)
    blocks = [one_hot[:, b * W : (b + 1) * W] for b in range(S // W)]
    upper = hot(
        lax.broadcasted_iota(jnp.int32, (W, W), 0)
        <= lax.broadcasted_iota(jnp.int32, (W, W), 1)
    )
    cum = nn(jnp.concatenate(blocks, axis=0).astype(BF), upper)
    before = jnp.zeros((E, 1), F32)
    places = []
    for b in range(S // W):
        part = cum[b * E : (b + 1) * E]
        places.append(
            jnp.sum(blocks[b] * (part + (before - 1.0)), axis=0, keepdims=True)
        )
        before = before + part[:, W - 1 : W]
    position = jnp.concatenate(places, axis=1).astype(jnp.int32)
    q = hot(lax.broadcasted_iota(jnp.int32, (CAP, S), 0) == position)
    q_ref[...] = q
    tgt = tgt_ref[...]
    tgt_hi = tgt.astype(BF).astype(F32)
    tgt_lo = tgt - tgt_hi
    texel = texel_ref[...]
    values = jnp.concatenate(
        [
            tgt_hi,
            tgt_lo,
            (texel % HI + 1).astype(F32),
            (tile_ref[...] * LO + texel // HI).astype(F32),
            (dir_ref[...] + 1).astype(F32),
            jnp.zeros((VROWS - 2 * OUTC - 3, S), F32),
        ],
        axis=0,
    )
    spread = jnp.concatenate(
        [jnp.where(mat == e, values, 0.0).astype(BF) for e in range(E)], axis=0
    )
    routed = nt(spread, q).astype(BF)
    for d in range(N):
        slot_send[d] = routed[d * L * VROWS : (d + 1) * L * VROWS]

    def slot_copy(k):
        peer = (me + k) % N
        return remote(
            slot_send.at[peer], slot_recv.at[me], slot_sems, (k - 1,), {"exp": peer}
        )

    for k in range(1, N):
        slot_copy(k).start()
    slot_recv[me] = slot_send[me]
    dg_acc[...] = jnp.zeros(dg_acc.shape, F32)
    for k in range(1, N):
        tex_copy(k).wait()
    for k in range(1, N):
        slot_copy(k).wait()

    def half_copy(e):
        return remote(hs_send.at[e], hs_recv.at[e], hs_sems, (e,), {"rep": mate})

    def expert(e, carry):
        layer_one = w1_ref[e]
        layer_two = w2_ref[e]
        layer_three = jnp.concatenate(
            [w3_ref[e], jnp.zeros((VROWS - OUTC, HID), BF)], axis=0
        )
        lat_part = jnp.concatenate([layer_one[:LAT]] * LO, axis=0)
        wide_one = jnp.concatenate([lat_part, layer_one[LAT:]], axis=0)

        def chunk(b, carry):
            width = SB * CAP
            v = jnp.concatenate(
                [
                    slot_recv[b * SB + i, pl.ds(pl.multiple_of(e * VROWS, VROWS), VROWS), :]
                    for i in range(SB)
                ],
                axis=1,
            ).astype(F32)
            target = v[:OUTC] + v[OUTC : 2 * OUTC]
            hi = v[2 * OUTC : 2 * OUTC + 1]
            tlo = v[2 * OUTC + 1 : 2 * OUTC + 2]
            di = v[2 * OUTC + 2 : 2 * OUTC + 3].astype(jnp.int32)
            hi = hi.astype(jnp.int32)
            tlo = tlo.astype(jnp.int32)
            tile = tlo // LO
            low = tlo % LO
            count = lax.broadcasted_iota(jnp.int32, (HI, width), 0) + 1
            hots = [hot(count == jnp.where(tile == t, hi, 0)) for t in range(T)]
            found = jnp.zeros((K, width), F32)
            for t in range(T):
                found += nn(tex[:, t].reshape(K, HI), hots[t])
            in_low = lax.broadcasted_iota(jnp.int32, (K, width), 0) // LAT == low
            found = jnp.where(in_low, found, 0.0).astype(BF)
            dir_hot = hot(lax.broadcasted_iota(jnp.int32, (NDIR, width), 0) + 1 == di)
            dir_part = tn(dirt_ref[...], dir_hot).astype(BF)
            x = jnp.concatenate([found, dir_part], axis=0)
            pre_one = tn(wide_one, x)
            sig_one = 0.5 * jnp.tanh(0.5 * pre_one) + 0.5
            act_one = (pre_one * sig_one).astype(BF)
            slope_one = sig_one * (1.0 + pre_one * (1.0 - sig_one))
            pre_two = tn(layer_two, act_one)
            sig_two = 0.5 * jnp.tanh(0.5 * pre_two) + 0.5
            act_two = (pre_two * sig_two).astype(BF)
            slope_two = sig_two * (1.0 + pre_two * (1.0 - sig_two))
            predicted = nn(layer_three, act_two)
            for i in range(SB):
                ps_send[b * SB + i, e] = predicted[:8, i * CAP : (i + 1) * CAP]
            misfit = (
                predicted
                - jnp.concatenate([target, jnp.zeros((VROWS - OUTC, width), F32)], axis=0)
            ).astype(BF)
            grad_three = nt(misfit, act_two)
            delta_two = (tn(layer_three, misfit) * slope_two).astype(BF)
            grad_two = nt(act_one, delta_two)
            delta_one = (nn(layer_two, delta_two) * slope_one).astype(BF)
            grad_one = nt(x, delta_one)
            rows = nn(lat_part, delta_one)
            rows = jnp.where(in_low, rows, 0.0).astype(BF)
            for t in range(T):
                dg_acc[t] += nt(rows, hots[t])
            g1_acc[...] += grad_one
            gfull[e, 2 * LAT : 2 * LAT + HID] += grad_two
            gfull[e, 2 * LAT + HID : 2 * LAT + HID + VROWS] += grad_three
            return carry

        g1_acc[...] = jnp.zeros(g1_acc.shape, F32)
        gfull[e] = jnp.zeros((CH, HID), F32)
        lax.fori_loop(0, N // SB, chunk, 0)
        lat_grad = g1_acc[0:LAT]
        for l in range(1, LO):
            lat_grad = lat_grad + g1_acc[l * LAT : (l + 1) * LAT]
        gfull[e, 0:LAT] = lat_grad
        gfull[e, LAT : LAT + DIRF] = g1_acc[K:]
        theirs = gfull[e, pl.ds(pl.multiple_of((1 - core) * (CH // 2), 8), CH // 2), :]
        hs_send[e] = theirs.astype(BF)
        half_copy(e).start()
        return carry

    lax.fori_loop(0, L, expert, 0)

    def pred_copy(k):
        peer = (me + k) % N
        return remote(ps_send.at[peer], ps_recv.at[me], ps_sems, (k - 1,), {"exp": peer})

    def dense_copy(k):
        peer = (me + k) % N
        return remote(dg_send.at[peer], dg_recv.at[me], dg_sems, (k - 1,), {"exp": peer})

    for k in range(1, N):
        pred_copy(k).start()
    ps_recv[me] = ps_send[me]
    for d in range(N):
        for t in range(T):
            dg_send[d, t] = dg_acc[t, d * PL : (d + 1) * PL].astype(BF)
    for k in range(1, N):
        dense_copy(k).start()

    def z_copy(k):
        there = (zi + k) % Z
        return remote(
            zs_send.at[there], zr_recv.at[zi], zr_sems, (k - 1,), {"rep": there * 2 + core}
        )

    def gather_copy(k):
        there = (zi + k) % Z
        return remote(
            fin.at[core, zi], fin.at[core, zi], ag_sems, (k - 1,), {"rep": there * 2 + core}
        )

    def forward_copy(k):
        owner = (zi + Z - k) % Z
        return remote(
            fin.at[core, owner], fin.at[core, owner], fw_sems, (k,), {"rep": mate}
        )

    for e in range(L):
        half_copy(e).wait()
        for z in range(Z):
            own = gfull[e, pl.ds(pl.multiple_of(core * (CH // 2) + z * RC, 8), RC), :]
            zs_send[z, e] = (own + hs_recv[e, z * RC : (z + 1) * RC].astype(F32)).astype(BF)
    for k in range(1, Z):
        z_copy(k).start()

    for k in range(1, N):
        dense_copy(k).wait()
    for t in range(T):
        grad = dg_acc[t, pl.ds(pl.multiple_of(me * PL, 8), PL), :]
        for k in range(1, N):
            grad = grad + dg_recv[(me + k) % N, t].astype(F32)
        for l in range(LOL):
            lanes = slice(l * HI, (l + 1) * HI)
            g = grad[l * LAT : (l + 1) * LAT]
            new_mean = decay_one * mean_ref[t, :, lanes] + (1.0 - decay_one) * g
            new_sq = decay_two * sq_ref[t, :, lanes] + (1.0 - decay_two) * g * g
            nmean_ref[t, :, lanes] = new_mean
            nsq_ref[t, :, lanes] = new_sq
            nlat_ref[t, :, lanes] = lat_ref[t, :, lanes] - step_rate * new_mean / (
                jnp.sqrt(new_sq) + epsilon
            )

    for k in range(1, Z):
        z_copy(k).wait()
    total = zs_send[zi].astype(F32)
    for k in range(1, Z):
        total = total + zr_recv[(zi + k) % Z].astype(F32)
    fin[core, zi] = total.astype(BF)
    for k in range(1, Z):
        gather_copy(k).start()
    forward_copy(0).start()

    for k in range(1, N):
        pred_copy(k).wait()
    slots = ps_recv[...].reshape(E * 8, CAP)
    slots_hi = slots.astype(BF)
    slots_lo = (slots - slots_hi.astype(F32)).astype(BF)
    back = nn(slots_hi, q_ref[...]) + nn(slots_lo, q_ref[...])
    mat = mat_ref[...]
    mine = jnp.zeros((8, S), F32)
    for e in range(E):
        mine = mine + jnp.where(mat == e, back[e * 8 : (e + 1) * 8], 0.0)
    pred_ref[...] = mine[:OUTC]

    for k in range(1, Z):
        gather_copy(k).wait()
        forward_copy(k).start()
    for k in range(Z):
        forward_copy(k).wait()
    for e in range(L):
        for h in range(2):
            for z in range(Z):
                start = (h * Z + z) * RC
                gfull[e, start : start + RC] = fin[h, z, e].astype(F32)
        g1_ref[e] = gfull[e, 0 : LAT + DIRF]
        g2_ref[e] = gfull[e, LAT + DIRF : LAT + DIRF + HID]
        g3_ref[e] = gfull[e, LAT + DIRF + HID : LAT + DIRF + HID + OUTC]


def on_device(N, R, *args):
    latents, _, _, weight_one, weight_two, weight_three, dir_table = args[:7]
    materials, tile_ids, texel_ids, dir_ids, targets = args[7:]
    T, LAT, texl = latents.shape
    L, width, HID = weight_one.shape
    OUTC = weight_three.shape[1]
    DIRF = dir_table.shape[1]
    S = materials.shape[0]
    E = L * N
    CAP = max(128, 2 * S // E)
    HI = min(256, texl)
    LOL = texl // HI
    LO = N * LOL
    Z = R // 2
    unit = 8 * R
    CH = -(-(width + HID + VROWS) // unit) * unit
    RC = CH // R
    K = LO * LAT
    cfg = dict(
        N=N, R=R, E=E, L=L, S=S, CAP=CAP, HI=HI, LOL=LOL, LO=LO, LAT=LAT, DIRF=DIRF,
        HID=HID, T=T, Z=Z, OUTC=OUTC, CH=CH, RC=RC, SB=2,
    )
    flat = [a.reshape(1, S) for a in (materials, tile_ids, texel_ids, dir_ids)]
    vmem = pl.BlockSpec(memory_space=pltpu.VMEM)
    outs = (
        jax.ShapeDtypeStruct(latents.shape, F32),
        jax.ShapeDtypeStruct(latents.shape, F32),
        jax.ShapeDtypeStruct(latents.shape, F32),
        jax.ShapeDtypeStruct(targets.shape, F32),
        jax.ShapeDtypeStruct(weight_one.shape, F32),
        jax.ShapeDtypeStruct(weight_two.shape, F32),
        jax.ShapeDtypeStruct(weight_three.shape, F32),
    )
    dma = pltpu.SemaphoreType.DMA
    scratch = [
        pltpu.VMEM((N, T, LOL * LAT, HI), BF),
        pltpu.VMEM((N, L * VROWS, CAP), BF),
        pltpu.VMEM((N, L * VROWS, CAP), BF),
        pltpu.VMEM((CAP, S), BF),
        pltpu.VMEM((N, L, 8, CAP), F32),
        pltpu.VMEM((N, L, 8, CAP), F32),
        pltpu.VMEM((T, K, HI), F32),
        pltpu.VMEM((N, T, LOL * LAT, HI), BF),
        pltpu.VMEM((N, T, LOL * LAT, HI), BF),
        pltpu.VMEM((K + DIRF, HID), F32),
        pltpu.VMEM((L, CH, HID), F32),
        pltpu.VMEM((L, CH // 2, HID), BF),
        pltpu.VMEM((L, CH // 2, HID), BF),
        pltpu.VMEM((Z, L, RC, HID), BF),
        pltpu.VMEM((Z, L, RC, HID), BF),
        pltpu.VMEM((2, Z, L, RC, HID), BF),
        dma((2, N - 1)),
        dma((2, N - 1)),
        dma((2, N - 1)),
        dma((2, N - 1)),
        dma((2, L)),
        dma((2, Z - 1)),
        dma((2, Z - 1)),
        dma((2, Z)),
    ]
    return pl.pallas_call(
        functools.partial(step_kernel, cfg),
        out_shape=outs,
        in_specs=[vmem] * 12,
        out_specs=tuple([vmem] * 7),
        scratch_shapes=scratch,
        compiler_params=pltpu.CompilerParams(
            collective_id=0, has_side_effects=True, vmem_limit_bytes=50 * 2**20
        ),
    )(*args[:7], *flat, targets)


def solution(mesh):
    tex = P("rep", None, "exp")
    own = P("exp", None, None)
    rows = P(("rep", "exp"))
    in_specs = (
        tex, tex, tex, own, own, own, P(), P(("rep", "exp"), None), rows, rows, rows,
        P(None, ("rep", "exp")),
    )
    out_specs = (tex, tex, tex, P(None, ("rep", "exp")), own, own, own)
    return jax.shard_map(
        functools.partial(on_device, mesh.shape["exp"], mesh.shape["rep"]),
        mesh=mesh,
        in_specs=in_specs,
        out_specs=out_specs,
        check_vma=False,
    )
```

time: 252 us -> 58.5 us (0.23)
  local copies, waits for them, and re-layouts: 128 us -> 10.9 us
  Pallas kernels: 0 us -> 45.9 us
  other arithmetic: 30.9 us -> 0 us
  matrix products: 27.1 us -> 0 us
  blocking collectives: 23.3 us -> 0 us
  starting transfers between devices: 15.6 us -> 0 us
  between operations: 15.9 us -> 0.7 us
  waiting for transfers between devices: 8.7 us -> 0 us
    unnamed x33 -> x30, local copies, waits for them, and re-layouts: 71.1 us -> 10.3 us
    pallas_call x0 -> x1, Pallas kernels: none -> 45.9 us  [on_device(): pl.pallas_call(functools.partial(step_kernel, cfg), out_shape=outs, in_sp...]
    dot_general x37 -> x0, matrix products: 27.1 us -> none  [the longest x4 5.92 us: expert_step(): pre_two = jnp.dot(act_one, layer_two, preferred_element_type=jnp.float32)]
    unnamed x4 -> x0, other arithmetic: 18.6 us -> none
    gather x3 -> x0, local copies, waits for them, and re-layouts: 16.8 us -> none  [the longest x2 11.3 us: on_device(): sample_latent = texture[tile_ids, :, texel_ids]]
    all_to_all x4 -> x0, starting transfers between devices: 15.3 us -> none  [the longest x1 5.19 us: on_device(): lax.all_to_all(send_targets.astype(jnp.bfloat16), 'exp', split_axis=1, co...]
    psum x1 -> x0, blocking collectives: 13.8 us -> none  [on_device(): lax.psum(grad_three.astype(jnp.bfloat16), 'rep').astype(jnp.float32)]
    scatter x2 -> x0, local copies, waits for them, and re-layouts: 12.2 us -> none  [the longest x1 6.1 us: on_device(): jnp.zeros((total_slots, OUTC), jnp.float32).at[slot_index].set(targets.T)]
  transfers between devices with their start and end apart: 6 -> 0, of which waited for: 2 -> 0; matrix products, arithmetic and copies ran while one was open for 48% -> 0% of each run, Pallas kernels for 0% -> 0%
where the time goes in v1:
time: 58.5 us; the launch traced here: 57.5 us
  Pallas kernels  45.9 us (78%)
  local copies, waits for them, and re-layouts  10.9 us (19%)
  between operations  0.7 us (1%)
    pallas_call x1, Pallas kernels, on_device(): pl.pallas_call(functools.partial(step_kernel, cfg), out_shape=outs, in_sp...  45.9 us
    unnamed x30, local copies, waits for them, and re-layouts  10.3 us

profile of v1, /device:TPU:0, one launch (start us, length us, event | category | flops | bytes accessed | tf_op | source)
XLA Modules:
  0.0 57.5 jit_solution(1521249592205776910)
XLA Ops:
  0.6 0.0 copy-start.10
  0.6 0.7 %copy.19.w3_ref = bf16[4,3,256]{2,1,0:T(4,128)(2,1)S(1)} copy(bf16[4,3,256]{2,0,1:T(4,128)(2,1)} %param.17) | data formatting | bytes 12288 | tf_op args[5]
  1.3 0.0 copy-done.10
  1.4 0.0 copy-start.5
  1.4 0.0 copy-start.6
  1.4 0.0 copy-start.7
  1.4 0.0 copy-start.8
  1.4 0.0 copy-start.9
  1.4 0.1 copy.20.dirt_ref
  1.5 0.6 %copy-done.5 = f32[3,2048]{1,0:T(4,128)S(1)} copy-done((f32[3,2048]{1,0:T(4,128)S(1)}, f32[3,2048]{1,0:T(4,128)}, u32[]{:S(2)}) %copy-start.5) | copy-done | bytes 24600
  2.1 0.0 copy-done.6
  2.1 0.0 copy-done.7
  2.1 0.0 copy-done.8
  2.1 0.0 copy-done.9
  2.1 0.0 copy-start
  2.1 1.0 %copy-done = bf16[4,256,256]{2,1,0:T(8,128)(2,1)S(1)} copy-done((bf16[4,256,256]{2,1,0:T(8,128)(2,1)S(1)}, bf16[4,256,256]{2,1,0:T(8,128)(2,1)}, u32[]{:S(2)}) %copy-start) | copy-done | bytes 524312
  3.2 0.0 copy-start.1
  3.2 0.9 %copy-done.1 = f32[2,32,512]{2,1,0:T(8,128)S(1)} copy-done((f32[2,32,512]{2,1,0:T(8,128)S(1)}, f32[2,32,512]{2,1,0:T(8,128)}, u32[]{:S(2)}) %copy-start.1) | copy-done | bytes 131096
  4.1 0.0 copy-start.2
  4.1 0.9 %copy-done.2 = f32[2,32,512]{2,1,0:T(8,128)S(1)} copy-done((f32[2,32,512]{2,1,0:T(8,128)S(1)}, f32[2,32,512]{2,1,0:T(8,128)}, u32[]{:S(2)}) %copy-start.2) | copy-done | bytes 131096
  5.0 0.0 copy-start.3
  5.0 0.9 %copy-done.3 = f32[2,32,512]{2,1,0:T(8,128)S(1)} copy-done((f32[2,32,512]{2,1,0:T(8,128)S(1)}, f32[2,32,512]{2,1,0:T(8,128)}, u32[]{:S(2)}) %copy-start.3) | copy-done | bytes 131096
  5.9 0.0 copy-start.4
  5.9 0.9 %copy-done.4 = bf16[4,64,256]{2,1,0:T(8,128)(2,1)S(1)} copy-done((bf16[4,64,256]{2,1,0:T(8,128)(2,1)S(1)}, bf16[4,64,256]{2,1,0:T(8,128)(2,1)}, u32[]{:S(2)}) %copy-start.4) | copy-done | bytes 131096
  6.8 45.9 %shard_map.171 = (f32[2,32,512]{2,1,0:T(8,128)S(1)}, f32[2,32,512]{2,1,0:T(8,128)S(1)}, f32[2,32,512]{2,1,0:T(8,128)S(1)}, f32[3,2048]{1,0:T(4,128)S(1)}, f32[4,...) custom-call(f32[2,32,512]{2,1,0:T(8,128)S(1)} %copy-done.1, ...), custom_call_target="tpu_custom_call" | custom-call | tf_op jit(solution)/shard_map/pallas_call | solution.py:430
  52.7 0.6 %copy.21 = f32[4,3,256]{2,0,1:T(4,128)} copy(f32[4,3,256]{2,1,0:T(4,128)S(1)} %get-tuple-element.13) | data formatting | bytes 24576 | tf_op jit(solution)/shard_map/pallas_call | solution.py:430
  53.3 0.7 %copy.28 = f32[2,32,512]{2,1,0:T(8,128)} copy(f32[2,32,512]{2,1,0:T(8,128)S(1)} %get-tuple-element.21) | data formatting | bytes 262144
  53.9 0.7 %copy.29 = f32[2,32,512]{2,1,0:T(8,128)} copy(f32[2,32,512]{2,1,0:T(8,128)S(1)} %get-tuple-element.22) | data formatting | bytes 262144
  54.6 0.7 %copy.30 = f32[2,32,512]{2,1,0:T(8,128)} copy(f32[2,32,512]{2,1,0:T(8,128)S(1)} %get-tuple-element.23) | data formatting | bytes 262144
  55.2 0.6 %copy.31 = f32[3,2048]{1,0:T(4,128)} copy(f32[3,2048]{1,0:T(4,128)S(1)} %get-tuple-element.24) | data formatting | bytes 49152
  55.9 0.7 %copy.32 = f32[4,64,256]{2,1,0:T(8,128)} copy(f32[4,64,256]{2,1,0:T(8,128)S(1)} %get-tuple-element.25) | data formatting | bytes 524288
  56.6 1.0 %copy.33 = f32[4,256,256]{2,1,0:T(8,128)} copy(f32[4,256,256]{2,1,0:T(8,128)S(1)} %get-tuple-element.26) | data formatting | bytes 2097152
Async XLA Ops:
  0.6 0.7 %copy-start.10 = (bf16[256,32]{0,1:T(8,128)(2,1)S(1)}, bf16[256,32]{0,1:T(8,128)(2,1)}, u32[]{:S(2)}) copy-start(bf16[256,32]{0,1:T(8,128)(2,1)} %param.18) | copy-start | bytes 49156
  1.4 0.8 %copy-start.5 = (f32[3,2048]{1,0:T(4,128)S(1)}, f32[3,2048]{1,0:T(4,128)}, u32[]{:S(2)}) copy-start(f32[3,2048]{1,0:T(4,128)} %tgt_ref.1) | copy-start | bytes 73732
  1.4 0.8 %copy-start.6 = (s32[2048,1]{0,1:T(1,128)S(1)}, s32[2048,1]{0,1:T(1,128)}, u32[]{:S(2)}) copy-start(s32[2048,1]{0,1:T(1,128)} %param.19) | copy-start | bytes 24580
  1.4 0.8 %copy-start.7 = (s32[2048]{0:T(1024)S(1)}, s32[2048]{0:T(1024)}, u32[]{:S(2)}) copy-start(s32[2048]{0:T(1024)} %param.20) | copy-start | bytes 24580
  1.4 0.7 %copy-start.8 = (s32[2048]{0:T(1024)S(1)}, s32[2048]{0:T(1024)}, u32[]{:S(2)}) copy-start(s32[2048]{0:T(1024)} %param.21) | copy-start | bytes 24580
  1.4 0.7 %copy-start.9 = (s32[2048]{0:T(1024)S(1)}, s32[2048]{0:T(1024)}, u32[]{:S(2)}) copy-start(s32[2048]{0:T(1024)} %param.22) | copy-start | bytes 24580
  2.1 1.0 %copy-start = (bf16[4,256,256]{2,1,0:T(8,128)(2,1)S(1)}, bf16[4,256,256]{2,1,0:T(8,128)(2,1)}, u32[]{:S(2)}) copy-start(bf16[4,256,256]{2,1,0:T(8,128)(2,1)} %w2_ref.1) | copy-start | bytes 1572868
  3.2 0.9 %copy-start.1 = (f32[2,32,512]{2,1,0:T(8,128)S(1)}, f32[2,32,512]{2,1,0:T(8,128)}, u32[]{:S(2)}) copy-start(f32[2,32,512]{2,1,0:T(8,128)} %lat_ref.1) | copy-start | bytes 393220
  4.1 0.9 %copy-start.2 = (f32[2,32,512]{2,1,0:T(8,128)S(1)}, f32[2,32,512]{2,1,0:T(8,128)}, u32[]{:S(2)}) copy-start(f32[2,32,512]{2,1,0:T(8,128)} %mean_ref.1) | copy-start | bytes 393220
  5.0 0.9 %copy-start.3 = (f32[2,32,512]{2,1,0:T(8,128)S(1)}, f32[2,32,512]{2,1,0:T(8,128)}, u32[]{:S(2)}) copy-start(f32[2,32,512]{2,1,0:T(8,128)} %sq_ref.1) | copy-start | bytes 393220
  5.9 0.9 %copy-start.4 = (bf16[4,64,256]{2,1,0:T(8,128)(2,1)S(1)}, bf16[4,64,256]{2,1,0:T(8,128)(2,1)}, u32[]{:S(2)}) copy-start(bf16[4,64,256]{2,1,0:T(8,128)(2,1)} %w1_ref.1) | copy-start | bytes 393220

commit v2 on v1

--- a/solution.py
+++ b/solution.py
@@ -35,57 +35,69 @@
 
 def step_kernel(
     cfg,
-    lat_ref,
-    mean_ref,
-    sq_ref,
-    w1_ref,
-    w2_ref,
-    w3_ref,
-    dirt_ref,
-    mat_ref,
-    tile_ref,
-    texel_ref,
-    dir_ref,
-    tgt_ref,
-    nlat_ref,
-    nmean_ref,
-    nsq_ref,
-    pred_ref,
-    g1_ref,
-    g2_ref,
-    g3_ref,
-    tex,
-    slot_send,
-    slot_recv,
-    q_ref,
-    ps_send,
-    ps_recv,
-    dg_acc,
-    dg_send,
-    dg_recv,
-    g1_acc,
-    gfull,
-    hs_send,
-    hs_recv,
-    zs_send,
-    zr_recv,
-    fin,
-    tex_sems,
-    slot_sems,
-    ps_sems,
-    dg_sems,
-    hs_sems,
-    zr_sems,
-    ag_sems,
-    fw_sems,
+    *refs,
 ):
+    hbm_in, hbm_out, rest = refs[:12], refs[12:19], refs[19:]
+    (
+        lat_ref,
+        mean_ref,
+        sq_ref,
+        w1_ref,
+        w2_ref,
+        w3_ref,
+        dirt_ref,
+        mat_ref,
+        tile_ref,
+        texel_ref,
+        dir_ref,
+        tgt_ref,
+    ) = rest[:12]
+    (
+        nlat_ref,
+        nmean_ref,
+        nsq_ref,
+        pred_ref,
+        g3_ref,
+    ) = rest[12:17]
+    (
+        tex,
+        slot_send,
+        slot_recv,
+        q_ref,
+        ps_send,
+        ps_recv,
+        dg_acc,
+        dg_send,
+        dg_recv,
+        g1_acc,
+        gfull,
+        hs_send,
+        hs_recv,
+        zs_send,
+        zr_recv,
+        fin,
+        w3p,
+        texture,
+        tex_sems,
+        slot_sems,
+        ps_sems,
+        dg_sems,
+        hs_sems,
+        zr_sems,
+        ag_sems,
+        fw_sems,
+        in_sems,
+        out_sems,
+        grad_sems,
+    ) = rest[17:]
     N, R, E, L = cfg["N"], cfg["R"], cfg["E"], cfg["L"]
     S, CAP, HI, LOL, LO = cfg["S"], cfg["CAP"], cfg["HI"], cfg["LOL"], cfg["LO"]
     LAT, DIRF, HID, T, Z = cfg["LAT"], cfg["DIRF"], cfg["HID"], cfg["T"], cfg["Z"]
     OUTC, CH, RC, SB = cfg["OUTC"], cfg["CH"], cfg["RC"], cfg["SB"]
-    NDIR = dirt_ref.shape[0]
+    NDIR = dirt_ref.shape[1]
     PL = LOL * LAT
     K = LO * LAT
+    first = LAT + DIRF + HID
     me = lax.axis_index("exp")
     rep = lax.axis_index("rep")
     core = rep % 2
@@ -102,6 +114,12 @@
             device_id_type=MESH,
         )
 
+    def load(i):
+        return pltpu.make_async_copy(hbm_in[i], rest[i], in_sems.at[i])
+
+    def save(i):
+        return pltpu.make_async_copy(rest[12 + min(i, 4)], hbm_out[i], out_sems.at[i])
+
     barrier = pltpu.get_barrier_semaphore()
     for k in range(1, N):
         pl.semaphore_signal(
@@ -115,6 +133,9 @@
             device_id={"rep": ((zi + k) % Z) * 2 + core},
             device_id_type=MESH,
         )
+    for i in (0, 7, 8, 9, 10, 11, 6, 3, 4, 5, 1, 2):
+        load(i).start()
+    load(0).wait()
     for t in range(T):
         for l in range(LOL):
             tex[me, t, l * LAT : (l + 1) * LAT, :] = lat_ref[
@@ -128,6 +149,8 @@
     for k in range(1, N):
         tex_copy(k).start()
 
+    for i in range(7, 12):
+        load(i).wait()
     mat = mat_ref[...]
     one_hot = jnp.where(
         lax.broadcasted_iota(jnp.int32, (E, S), 0) == mat, 1.0, 0.0
@@ -182,20 +205,73 @@
         slot_copy(k).start()
     slot_recv[me] = slot_send[me]
     dg_acc[...] = jnp.zeros(dg_acc.shape, F32)
+    for i in range(1, 7):
+        load(i).wait()
+    colour = w3_ref[...].astype(F32)
+    for e in range(L):
+        w3p[e] = jnp.concatenate(
+            [colour[c, e : e + 1] for c in range(OUTC)]
+            + [jnp.zeros((VROWS - OUTC, HID), F32)],
+            axis=0,
+        ).astype(BF)
     for k in range(1, N):
         tex_copy(k).wait()
+    for t in range(T):
+        for d in range(N):
+            texture[d * PL : (d + 1) * PL, t * HI : (t + 1) * HI] = tex[d, t]
     for k in range(1, N):
         slot_copy(k).wait()
 
     def half_copy(e):
         return remote(hs_send.at[e], hs_recv.at[e], hs_sems, (e,), {"rep": mate})
+
+    def z_copy(e, k):
+        there = (zi + k) % Z
+        return remote(
+            zs_send.at[e, there],
+            zr_recv.at[e, zi],
+            zr_sems,
+            (e, k - 1),
+            {"rep": there * 2 + core},
+        )
+
+    def gather_copy(e, k):
+        there = (zi + k) % Z
+        piece = fin.at[e, core, zi]
+        return remote(piece, piece, ag_sems, (e, k - 1), {"rep": there * 2 + core})
+
+    def forward_copy(e, k):
+        piece = fin.at[e, core, (zi + Z - k) % Z]
+        return remote(piece, piece, fw_sems, (e, k), {"rep": mate})
+
+    def halves(e):
+        half_copy(e).wait()
+        for z in range(Z):
+            own = gfull[e, pl.ds(pl.multiple_of(core * (CH // 2) + z * RC, 8), RC), :]
+            zs_send[e, z] = (own + hs_recv[e, z].astype(F32)).astype(BF)
+        for k in range(1, Z):
+            z_copy(e, k).start()
+
+    def parts(e):
+        for k in range(1, Z):
+            z_copy(e, k).wait()
+        total = zs_send[e, zi].astype(F32)
+        for k in range(1, Z):
+            total = total + zr_recv[e, (zi + k) % Z].astype(F32)
+        fin[e, core, zi] = total.astype(BF)
+        for k in range(1, Z):
+            gather_copy(e, k).start()
+        forward_copy(e, 0).start()
+
+    def returns(e):
+        for k in range(1, Z):
+            gather_copy(e, k).wait()
+            forward_copy(e, k).start()
 
     def expert(e, carry):
         layer_one = w1_ref[e]
         layer_two = w2_ref[e]
-        layer_three = jnp.concatenate(
-            [w3_ref[e], jnp.zeros((VROWS - OUTC, HID), BF)], axis=0
-        )
+        layer_three = w3p[e]
         lat_part = jnp.concatenate([layer_one[:LAT]] * LO, axis=0)
         wide_one = jnp.concatenate([lat_part, layer_one[LAT:]], axis=0)
 
@@ -218,22 +294,32 @@
             low = tlo % LO
             count = lax.broadcasted_iota(jnp.int32, (HI, width), 0) + 1
             hots = [hot(count == jnp.where(tile == t, hi, 0)) for t in range(T)]
-            found = jnp.zeros((K, width), F32)
-            for t in range(T):
-                found += nn(tex[:, t].reshape(K, HI), hots[t])
-            in_low = lax.broadcasted_iota(jnp.int32, (K, width), 0) // LAT == low
-            found = jnp.where(in_low, found, 0.0).astype(BF)
+            hots = jnp.concatenate(hots, axis=0)
+            spot = jnp.broadcast_to(low, (LAT, width))
+
+            def in_place(wide):
+                return jnp.concatenate(
+                    [
+                        jnp.where(spot == l, wide[l * LAT : (l + 1) * LAT], 0.0).astype(BF)
+                        for l in range(LO)
+                    ],
+                    axis=0,
+                )
+
+            found = in_place(nn(texture[...], hots))
             dir_hot = hot(lax.broadcasted_iota(jnp.int32, (NDIR, width), 0) + 1 == di)
-            dir_part = tn(dirt_ref[...], dir_hot).astype(BF)
+            dir_part = nn(dirt_ref[...], dir_hot).astype(BF)
             x = jnp.concatenate([found, dir_part], axis=0)
             pre_one = tn(wide_one, x)
             sig_one = 0.5 * jnp.tanh(0.5 * pre_one) + 0.5
-            act_one = (pre_one * sig_one).astype(BF)
-            slope_one = sig_one * (1.0 + pre_one * (1.0 - sig_one))
+            silu_one = pre_one * sig_one
+            act_one = silu_one.astype(BF)
+            slope_one = sig_one + silu_one * (1.0 - sig_one)
             pre_two = tn(layer_two, act_one)
             sig_two = 0.5 * jnp.tanh(0.5 * pre_two) + 0.5
-            act_two = (pre_two * sig_two).astype(BF)
-            slope_two = sig_two * (1.0 + pre_two * (1.0 - sig_two))
+            silu_two = pre_two * sig_two
+            act_two = silu_two.astype(BF)
+            slope_two = sig_two + silu_two * (1.0 - sig_two)
             predicted = nn(layer_three, act_two)
             for i in range(SB):
                 ps_send[b * SB + i, e] = predicted[:8, i * CAP : (i + 1) * CAP]
@@ -246,26 +332,37 @@
             grad_two = nt(act_one, delta_two)
             delta_one = (nn(layer_two, delta_two) * slope_one).astype(BF)
             grad_one = nt(x, delta_one)
-            rows = nn(lat_part, delta_one)
-            rows = jnp.where(in_low, rows, 0.0).astype(BF)
-            for t in range(T):
-                dg_acc[t] += nt(rows, hots[t])
-            g1_acc[...] += grad_one
-            gfull[e, 2 * LAT : 2 * LAT + HID] += grad_two
-            gfull[e, 2 * LAT + HID : 2 * LAT + HID + VROWS] += grad_three
+            dg_acc[...] += nt(in_place(nn(lat_part, delta_one)), hots)
+            two, three = slice(LAT + DIRF, first), slice(first, first + VROWS)
+            if N == SB:
+                g1_acc[...] = grad_one
+                gfull[e, two] = grad_two
+                gfull[e, three] = grad_three
+            else:
+                g1_acc[...] += grad_one
+                gfull[e, two] += grad_two
+                gfull[e, three] += grad_three
             return carry
 
-        g1_acc[...] = jnp.zeros(g1_acc.shape, F32)
-        gfull[e] = jnp.zeros((CH, HID), F32)
-        lax.fori_loop(0, N // SB, chunk, 0)
+        gfull[e, first:] = jnp.zeros((CH - first, HID), F32)
+        if N == SB:
+            chunk(0, 0)
+        else:
+            g1_acc[...] = jnp.zeros(g1_acc.shape, F32)
+            gfull[e, :first] = jnp.zeros((first, HID), F32)
+            lax.fori_loop(0, N // SB, chunk, 0)
         lat_grad = g1_acc[0:LAT]
         for l in range(1, LO):
             lat_grad = lat_grad + g1_acc[l * LAT : (l + 1) * LAT]
         gfull[e, 0:LAT] = lat_grad
         gfull[e, LAT : LAT + DIRF] = g1_acc[K:]
-        theirs = gfull[e, pl.ds(pl.multiple_of((1 - core) * (CH // 2), 8), CH // 2), :]
-        hs_send[e] = theirs.astype(BF)
+        for z in range(Z):
+            their = (1 - core) * (CH // 2) + z * RC
+            hs_send[e, z] = gfull[e, pl.ds(pl.multiple_of(their, 8), RC), :].astype(BF)
         half_copy(e).start()
+        pl.when(e >= 1)(lambda: halves(e - 1))
+        pl.when(e >= 2)(lambda: parts(e - 2))
+        pl.when(e >= 3)(lambda: returns(e - 3))
         return carry
 
     lax.fori_loop(0, L, expert, 0)
@@ -283,40 +380,46 @@
     ps_recv[me] = ps_send[me]
     for d in range(N):
         for t in range(T):
-            dg_send[d, t] = dg_acc[t, d * PL : (d + 1) * PL].astype(BF)
+            dg_send[d, t] = dg_acc[
+                d * PL : (d + 1) * PL, t * HI : (t + 1) * HI
+            ].astype(BF)
     for k in range(1, N):
         dense_copy(k).start()
 
-    def z_copy(k):
-        there = (zi + k) % Z
-        return remote(
-            zs_send.at[there], zr_recv.at[zi], zr_sems, (k - 1,), {"rep": there * 2 + core}
-        )
-
-    def gather_copy(k):
-        there = (zi + k) % Z
-        return remote(
-            fin.at[core, zi], fin.at[core, zi], ag_sems, (k - 1,), {"rep": there * 2 + core}
-        )
-
-    def forward_copy(k):
-        owner = (zi + Z - k) % Z
-        return remote(
-            fin.at[core, owner], fin.at[core, owner], fw_sems, (k,), {"rep": mate}
-        )
-
-    for e in range(L):
-        half_copy(e).wait()
-        for z in range(Z):
-            own = gfull[e, pl.ds(pl.multiple_of(core * (CH // 2) + z * RC, 8), RC), :]
-            zs_send[z, e] = (own + hs_recv[e, z * RC : (z + 1) * RC].astype(F32)).astype(BF)
-    for k in range(1, Z):
-        z_copy(k).start()
+    def save_one(e):
+        return pltpu.make_async_copy(
+            gfull.at[e, 0 : LAT + DIRF], hbm_out[4].at[e], grad_sems.at[0, e]
+        )
+
+    def save_two(e):
+        return pltpu.make_async_copy(
+            gfull.at[e, LAT + DIRF : first], hbm_out[5].at[e], grad_sems.at[1, e]
+        )
+
+    def finish(e):
+        for k in range(Z):
+            forward_copy(e, k).wait()
+        for h in range(2):
+            for z in range(Z):
+                start = (h * Z + z) * RC
+                gfull[e, start : start + RC] = fin[e, h, z].astype(F32)
+        save_one(e).start()
+        save_two(e).start()
+
+    halves(L - 1)
+    if L > 1:
+        parts(L - 2)
+    if L > 2:
+        returns(L - 3)
+    for e in range(L - 3):
+        finish(e)
 
     for k in range(1, N):
         dense_copy(k).wait()
     for t in range(T):
-        grad = dg_acc[t, pl.ds(pl.multiple_of(me * PL, 8), PL), :]
+        grad = dg_acc[
+            pl.ds(pl.multiple_of(me * PL, 8), PL), t * HI : (t + 1) * HI
+        ]
         for k in range(1, N):
             grad = grad + dg_recv[(me + k) % N, t].astype(F32)
         for l in range(LOL):
@@ -330,15 +433,13 @@
                 jnp.sqrt(new_sq) + epsilon
             )
 
-    for k in range(1, Z):
-        z_copy(k).wait()
-    total = zs_send[zi].astype(F32)
-    for k in range(1, Z):
-        total = total + zr_recv[(zi + k) % Z].astype(F32)
-    fin[core, zi] = total.astype(BF)
-    for k in range(1, Z):
-        gather_copy(k).start()
-    forward_copy(0).start()
+    for i in range(3):
+        save(i).start()
+    parts(L - 1)
+    if L > 1:
+        returns(L - 2)
+    if L > 2:
+        finish(L - 3)
 
     for k in range(1, N):
         pred_copy(k).wait()
@@ -352,19 +453,20 @@
         mine = mine + jnp.where(mat == e, back[e * 8 : (e + 1) * 8], 0.0)
     pred_ref[...] = mine[:OUTC]
 
-    for k in range(1, Z):
-        gather_copy(k).wait()
-        forward_copy(k).start()
-    for k in range(Z):
-        forward_copy(k).wait()
+    save(3).start()
+    if L > 1:
+        finish(L - 2)
+    returns(L - 1)
+    finish(L - 1)
     for e in range(L):
-        for h in range(2):
-            for z in range(Z):
-                start = (h * Z + z) * RC
-                gfull[e, start : start + RC] = fin[h, z, e].astype(F32)
-        g1_ref[e] = gfull[e, 0 : LAT + DIRF]
-        g2_ref[e] = gfull[e, LAT + DIRF : LAT + DIRF + HID]
-        g3_ref[e] = gfull[e, LAT + DIRF + HID : LAT + DIRF + HID + OUTC]
+        for c in range(OUTC):
+            g3_ref[c, e : e + 1] = gfull[e, first + c : first + c + 1]
+    save(6).start()
+    for i in (0, 1, 2, 3, 6):
+        save(i).wait()
+    for e in range(L):
+        save_one(e).wait()
+        save_two(e).wait()
 
 
 def on_device(N, R, *args):
@@ -373,6 +475,7 @@
     T, LAT, texl = latents.shape
     L, width, HID = weight_one.shape
     OUTC = weight_three.shape[1]
+    weight_three = weight_three.transpose(1, 0, 2)
     DIRF = dir_table.shape[1]
     S = materials.shape[0]
     E = L * N
@@ -387,10 +490,12 @@
     K = LO * LAT
     cfg = dict(
         N=N, R=R, E=E, L=L, S=S, CAP=CAP, HI=HI, LOL=LOL, LO=LO, LAT=LAT, DIRF=DIRF,
-        HID=HID, T=T, Z=Z, OUTC=OUTC, CH=CH, RC=RC, SB=2,
+        HID=HID, T=T, Z=Z, OUTC=OUTC, CH=CH, RC=RC, SB=min(4, N),
     )
     flat = [a.reshape(1, S) for a in (materials, tile_ids, texel_ids, dir_ids)]
-    vmem = pl.BlockSpec(memory_space=pltpu.VMEM)
+    hbm = pl.BlockSpec(memory_space=pltpu.HBM)
+    operands = (*args[:5], weight_three, dir_table.T, *flat, targets)
+    operands = tuple(pltpu.with_memory_space_constraint(a, pltpu.HBM) for a in operands)
     outs = (
         jax.ShapeDtypeStruct(latents.shape, F32),
         jax.ShapeDtypeStruct(latents.shape, F32),
@@ -401,42 +506,49 @@
         jax.ShapeDtypeStruct(weight_three.shape, F32),
     )
     dma = pltpu.SemaphoreType.DMA
-    scratch = [
+    scratch = [pltpu.VMEM(a.shape, a.dtype) for a in (*operands, *outs[:4], outs[6])]
+    scratch += [
         pltpu.VMEM((N, T, LOL * LAT, HI), BF),
         pltpu.VMEM((N, L * VROWS, CAP), BF),
         pltpu.VMEM((N, L * VROWS, CAP), BF),
         pltpu.VMEM((CAP, S), BF),
         pltpu.VMEM((N, L, 8, CAP), F32),
         pltpu.VMEM((N, L, 8, CAP), F32),
-        pltpu.VMEM((T, K, HI), F32),
+        pltpu.VMEM((K, T * HI), F32),
         pltpu.VMEM((N, T, LOL * LAT, HI), BF),
         pltpu.VMEM((N, T, LOL * LAT, HI), BF),
         pltpu.VMEM((K + DIRF, HID), F32),
         pltpu.VMEM((L, CH, HID), F32),
-        pltpu.VMEM((L, CH // 2, HID), BF),
-        pltpu.VMEM((L, CH // 2, HID), BF),
-        pltpu.VMEM((Z, L, RC, HID), BF),
-        pltpu.VMEM((Z, L, RC, HID), BF),
-        pltpu.VMEM((2, Z, L, RC, HID), BF),
+        pltpu.VMEM((L, Z, RC, HID), BF),
+        pltpu.VMEM((L, Z, RC, HID), BF),
+        pltpu.VMEM((L, Z, RC, HID), BF),
+        pltpu.VMEM((L, Z, RC, HID), BF),
+        pltpu.VMEM((L, 2, Z, RC, HID), BF),
+        pltpu.VMEM((L, VROWS, HID), BF),
+        pltpu.VMEM((K, T * HI), BF),
         dma((2, N - 1)),
         dma((2, N - 1)),
         dma((2, N - 1)),
         dma((2, N - 1)),
         dma((2, L)),
-        dma((2, Z - 1)),
-        dma((2, Z - 1)),
-        dma((2, Z)),
+        dma((2, L, Z - 1)),
+        dma((2, L, Z - 1)),
+        dma((2, L, Z)),
+        dma((12,)),
+        dma((7,)),
+        dma((2, L)),
     ]
-    return pl.pallas_call(
+    results = pl.pallas_call(
         functools.partial(step_kernel, cfg),
-        out_shape=outs,
-        in_specs=[vmem] * 12,
-        out_specs=tuple([vmem] * 7),
+        out_shape=tuple(pltpu.HBM(a.shape, a.dtype) for a in outs),
+        in_specs=[hbm] * 12,
+        out_specs=tuple([hbm] * 7),
         scratch_shapes=scratch,
         compiler_params=pltpu.CompilerParams(
             collective_id=0, has_side_effects=True, vmem_limit_bytes=50 * 2**20
         ),
-    )(*args[:7], *flat, targets)
+    )(*operands)
+    return (*results[:6], results[6].transpose(1, 0, 2))
 
 
 def solution(mesh):

time: 58.5 us -> 50.5 us (0.86); the launches traced: 57.5 us -> 50.2 us
  Pallas kernels: 45.9 us -> 40.1 us
  local copies, waits for them, and re-layouts: 10.9 us -> 9.42 us
    pallas_call x1, Pallas kernels: 45.9 us -> 40.1 us  [on_device(): pl.pallas_call(functools.partial(step_kernel, cfg), out_shape=tuple((pltp...]
    unnamed x30 -> x11, local copies, waits for them, and re-layouts: 10.3 us -> 9.42 us
    pallas_call x1 -> x0, local copies, waits for them, and re-layouts: 0.6 us -> none  [on_device(): pl.pallas_call(functools.partial(step_kernel, cfg), out_shape=outs, in_sp...]
where the time goes in v2:
time: 50.5 us; the launch traced here: 50.2 us
  Pallas kernels  40.1 us (79%)
  local copies, waits for them, and re-layouts  9.42 us (19%)
  between operations  0.66 us (1%)
    pallas_call x1, Pallas kernels, on_device(): pl.pallas_call(functools.partial(step_kernel, cfg), out_shape=tuple((pltp...  40.1 us
    unnamed x11, local copies, waits for them, and re-layouts  9.42 us

profile of v2, /device:TPU:0, one launch (start us, length us, event | category | flops | bytes accessed | tf_op | source)
XLA Modules:
  0.0 50.2 jit_solution(12045337106825519844)
XLA Ops:
  0.6 40.1 %shard_map.171 = (f32[2,32,512]{2,1,0:T(8,128)}, f32[2,32,512]{2,1,0:T(8,128)}, f32[2,32,512]{2,1,0:T(8,128)}, f32[3,2048]{1,0:T(4,128)}, f32[4,64,256]{2,1,0:T(...) custom-call(f32[2,32,512]{2,1,0:T(8,128)} %refs_0_.1, f32[2,32,512]{2,1,0:T(8,128)} %refs_1_.1, ...), custom_call_target="tpu_custom_call" | custom-call | tf_op jit(solution)/shard_map/pallas_call | solution.py:541
  40.8 0.0 copy-start
  40.8 1.7 %copy.26 = f32[2,32,512]{2,1,0:T(8,128)} copy(f32[2,32,512]{2,1,0:T(8,128)} %get-tuple-element.28) | data formatting | bytes 262144
  42.4 1.6 %copy.27 = f32[2,32,512]{2,1,0:T(8,128)} copy(f32[2,32,512]{2,1,0:T(8,128)} %get-tuple-element.29) | data formatting | bytes 262144
  44.0 1.6 %copy.28 = f32[2,32,512]{2,1,0:T(8,128)} copy(f32[2,32,512]{2,1,0:T(8,128)} %get-tuple-element.30) | data formatting | bytes 262144
  45.6 1.4 %copy.29 = f32[3,2048]{1,0:T(4,128)} copy(f32[3,2048]{1,0:T(4,128)} %get-tuple-element.31) | data formatting | bytes 49152
  46.9 1.7 %copy.30 = f32[4,64,256]{2,1,0:T(8,128)} copy(f32[4,64,256]{2,1,0:T(8,128)} %get-tuple-element.32) | data formatting | bytes 524288
  48.6 0.0 copy-done
  48.6 0.0 copy-start.1
  48.6 1.0 %copy.31 = f32[4,256,256]{2,1,0:T(8,128)} copy(f32[4,256,256]{2,1,0:T(8,128)S(1)} %copy-done) | data formatting | bytes 2097152
  49.6 0.0 copy-done.1
  49.6 0.6 %copy.32 = f32[4,3,256]{2,0,1:T(4,128)} copy(f32[4,3,256]{2,0,1:T(4,128)S(1)} %bitcast.8) | data formatting | bytes 24576
Async XLA Ops:
  40.8 7.9 %copy-start = (f32[4,256,256]{2,1,0:T(8,128)S(1)}, f32[4,256,256]{2,1,0:T(8,128)}, u32[]{:S(2)}) copy-start(f32[4,256,256]{2,1,0:T(8,128)} %get-tuple-element.33) | copy-start | bytes 3145732
  48.6 1.0 %copy-start.1 = (f32[3,4,256]{2,1,0:T(4,128)S(1)}, f32[3,4,256]{2,1,0:T(4,128)}, u32[]{:S(2)}) copy-start(f32[3,4,256]{2,1,0:T(4,128)} %get-tuple-element.20) | copy-start | bytes 36868

commit v3 on v2

--- a/solution.py
+++ b/solution.py
@@ -141,11 +141,10 @@
             tex[me, t, l * LAT : (l + 1) * LAT, :] = lat_ref[
                 t, :, l * HI : (l + 1) * HI
             ].astype(BF)
-    pl.semaphore_wait(barrier, (N - 1) + 1 + (Z - 1))
-
     def tex_copy(k):
         return remote(tex.at[me], tex.at[me], tex_sems, (k - 1,), {"exp": (me + k) % N})
 
+    pl.semaphore_wait(barrier, (N - 1) + 1 + (Z - 1))
     for k in range(1, N):
         tex_copy(k).start()
 
@@ -375,17 +374,6 @@
         peer = (me + k) % N
         return remote(dg_send.at[peer], dg_recv.at[me], dg_sems, (k - 1,), {"exp": peer})
 
-    for k in range(1, N):
-        pred_copy(k).start()
-    ps_recv[me] = ps_send[me]
-    for d in range(N):
-        for t in range(T):
-            dg_send[d, t] = dg_acc[
-                d * PL : (d + 1) * PL, t * HI : (t + 1) * HI
-            ].astype(BF)
-    for k in range(1, N):
-        dense_copy(k).start()
-
     def save_one(e):
         return pltpu.make_async_copy(
             gfull.at[e, 0 : LAT + DIRF], hbm_out[4].at[e], grad_sems.at[0, e]
@@ -406,6 +394,16 @@
         save_one(e).start()
         save_two(e).start()
 
+    for d in range(N):
+        for t in range(T):
+            dg_send[d, t] = dg_acc[
+                d * PL : (d + 1) * PL, t * HI : (t + 1) * HI
+            ].astype(BF)
+    for k in range(1, N):
+        dense_copy(k).start()
+    for k in range(1, N):
+        pred_copy(k).start()
+    ps_recv[me] = ps_send[me]
     halves(L - 1)
     if L > 1:
         parts(L - 2)
@@ -441,6 +439,9 @@
     if L > 2:
         finish(L - 3)
 
+    if L > 1:
+        finish(L - 2)
+    returns(L - 1)
     for k in range(1, N):
         pred_copy(k).wait()
     slots = ps_recv[...].reshape(E * 8, CAP)
@@ -454,9 +455,6 @@
     pred_ref[...] = mine[:OUTC]
 
     save(3).start()
-    if L > 1:
-        finish(L - 2)
-    returns(L - 1)
     finish(L - 1)
     for e in range(L):
         for c in range(OUTC):
@@ -540,7 +538,7 @@
     ]
     results = pl.pallas_call(
         functools.partial(step_kernel, cfg),
-        out_shape=tuple(pltpu.HBM(a.shape, a.dtype) for a in outs),
+        out_shape=outs,
         in_specs=[hbm] * 12,
         out_specs=tuple([hbm] * 7),
         scratch_shapes=scratch,

time: 50.5 us -> 45.2 us (0.90)
  local copies, waits for them, and re-layouts: 9.42 us -> 4.85 us
  Pallas kernels: 40.1 us -> 39.5 us
    unnamed x11 -> x7, local copies, waits for them, and re-layouts: 9.42 us -> 4.85 us
    pallas_call x1, Pallas kernels: 40.1 us -> 39.5 us  [on_device(): pl.pallas_call(functools.partial(step_kernel, cfg), out_shape=outs, in_sp...]
where the time goes in v3:
time: 45.2 us; the launch traced here: 45 us
  Pallas kernels  39.5 us (87%)
  local copies, waits for them, and re-layouts  4.85 us (11%)
  between operations  0.65 us (1%)
    pallas_call x1, Pallas kernels, on_device(): pl.pallas_call(functools.partial(step_kernel, cfg), out_shape=outs, in_sp...  39.5 us
    unnamed x7, local copies, waits for them, and re-layouts  4.85 us

profile of v3, /device:TPU:0, one launch (start us, length us, event | category | flops | bytes accessed | tf_op | source)
XLA Modules:
  0.0 45.0 jit_solution(14488643066140179033)
XLA Ops:
  0.6 39.5 %shard_map.171 = (f32[2,32,512]{2,1,0:T(8,128)S(1)}, f32[2,32,512]{2,1,0:T(8,128)S(1)}, f32[2,32,512]{2,1,0:T(8,128)S(1)}, f32[3,2048]{1,0:T(4,128)S(1)}, f32[4,...) custom-call(f32[2,32,512]{2,1,0:T(8,128)} %refs_0_.1, f32[2,32,512]{2,1,0:T(8,128)} %refs_1_.1, ...), custom_call_target="tpu_custom_call" | custom-call | tf_op jit(solution)/shard_map/pallas_call | solution.py:539
  40.2 0.7 %copy.26 = f32[2,32,512]{2,1,0:T(8,128)} copy(f32[2,32,512]{2,1,0:T(8,128)S(1)} %get-tuple-element.28) | data formatting | bytes 262144
  40.8 0.7 %copy.27 = f32[2,32,512]{2,1,0:T(8,128)} copy(f32[2,32,512]{2,1,0:T(8,128)S(1)} %get-tuple-element.29) | data formatting | bytes 262144
  41.5 0.7 %copy.28 = f32[2,32,512]{2,1,0:T(8,128)} copy(f32[2,32,512]{2,1,0:T(8,128)S(1)} %get-tuple-element.30) | data formatting | bytes 262144
  42.1 0.6 %copy.29 = f32[3,2048]{1,0:T(4,128)} copy(f32[3,2048]{1,0:T(4,128)S(1)} %get-tuple-element.31) | data formatting | bytes 49152
  42.7 0.7 %copy.30 = f32[4,64,256]{2,1,0:T(8,128)} copy(f32[4,64,256]{2,1,0:T(8,128)S(1)} %get-tuple-element.32) | data formatting | bytes 524288
  43.5 1.0 %copy.31 = f32[4,256,256]{2,1,0:T(8,128)} copy(f32[4,256,256]{2,1,0:T(8,128)S(1)} %get-tuple-element.33) | data formatting | bytes 2097152
  44.4 0.6 %copy.32 = f32[4,3,256]{2,0,1:T(4,128)} copy(f32[4,3,256]{2,0,1:T(4,128)S(1)} %bitcast.7) | data formatting | bytes 24576
